TPU v7x, 256 devices: a 2x2x32 block of a 4x8x32 slice. The times are simulated.
256 devices in a mesh: groups: 4 (over x, y), row: 64 (over z, core).
Axes of the slice: x: 2, y: 2, z: 32, core: 2. Of those that a mesh axis runs over, the one named last changes fastest.
The devices are a block of a 4x8x32 slice.
Arguments:
- factor_b: bfloat16 [64, 1048576], P(None, ('groups', 'row')), parts along dimension 1, may hold values from -12 to 12
- factor_c: bfloat16 [64, 1048576], P(None, ('groups', 'row')), parts along dimension 1, may hold values from -12 to 12
- sample_j: int32 [2097152], P(('groups', 'row')), parts along dimension 0, may hold values from 0 to 262143, as said below
- sample_k: int32 [64, 256, 128], P(None, ('groups', 'row')), parts along dimension 1, may hold values from 0 to 262143, as said below
- sample_weight: float32 [2097152], P(('groups', 'row')), parts along dimension 0, may hold values from 0.5 to 3.5
- block_values: bfloat16 [256, 64, 4, 4, 128], P(('groups', 'row')), parts along dimension 0, may hold values from -24 to 24
- block_sample: int32 [256, 64, 4, 4], P(('groups', 'row')), parts along dimension 0, may hold values from 0 to 8191
- block_count: int32 [256, 64, 4, 4], P(('groups', 'row')), parts along dimension 0, may hold values from 0 to 128, as said below
Outputs:
- factor_new: bfloat16 [64, 131072], P(None, ('groups', 'row')), parts along dimension 1
- scales: float32 [256], P('groups'), parts along dimension 0
There are 4 independent parts, one for each index of `groups`. A program takes and returns all parts, laid end to end along the dimension named above; each array names one. Nothing has to cross between parts.
Inputs may be any that keep to these rules, and one draw needn't show every extreme that they name: sample_j[s] lies in rows s // 8192 * 4096 to s // 8192 * 4096 + 4095. sample_k[d, e, i] is the third-mode index of sample d * 8192 + e * 128 + i and lies in rows e * 4096 to e * 4096 + 4095. `block_count`: 0 marks an empty slot; slot [p, p, 0, 0] holds 128 for every p.
All inputs are finite; a program needn't handle non-finite values.
Results may differ from a plain program's by a relative error of at most 0.0051.
Values may be sent and summed in bfloat16 or wider, within the bound.
A program may use at most 64 MiB of HBM per device.

v0:
```python
import jax
import jax.numpy as jnp
from jax import lax
from jax.sharding import Mesh
from jax.sharding import PartitionSpec as P

ROW = ("row_0", "row_1")
GROUPS_ROW = ("groups", "row_0", "row_1")


def by_axis(x, axes):
    for axis in axes:
        x = lax.psum(x, axis)
    return x


def sent_together(arrays, axis, split_dim, concat_dim, along):
    both = jnp.concatenate(arrays, axis=along)
    result, at, finished = (
        lax.all_to_all(both, axis, split_axis=split_dim, concat_axis=concat_dim, tiled=True),
        0,
        [],
    )
    for a in arrays:
        finished.append(lax.slice_in_dim(result, at, at + a.shape[along], axis=along))
        at += a.shape[along]
    return tuple(finished)


def from_everyone(x, axis):
    devices = lax.axis_size(axis)
    return lax.all_to_all(jnp.broadcast_to(x[None], (devices, *x.shape)), axis, 0, 0, tiled=True)


def over_copies(x, axis):
    return from_everyone(x, axis).sum(axis=0)


def shards(
    factor_b, factor_c, sample_j, sample_k, sample_weight, block_values, block_sample, block_count
):
    rank_width = factor_b.shape[0]
    device_count = lax.axis_size(ROW)
    device_index = lax.axis_index(ROW)
    b_columns = jnp.take(factor_b, sample_j - device_index * factor_b.shape[1], axis=1)
    c_local = sample_k.reshape(-1) - device_index * factor_c.shape[1]
    c_outgoing = jnp.take(factor_c, c_local, axis=1).reshape(rank_width, device_count, -1)
    c_columns = lax.all_to_all(c_outgoing, ROW, split_axis=1, concat_axis=1, tiled=True).reshape(
        rank_width, -1
    )
    sketch = sample_weight[None, :] * b_columns.astype(jnp.float32) * c_columns.astype(jnp.float32)
    gram_local = jnp.dot(sketch, sketch.T, precision=lax.Precision.HIGHEST)
    live_local = jnp.sum(block_count.astype(jnp.float32))
    gram_matrix, live_total = (by_axis(gram_local, ROW), by_axis(live_local, ROW))
    weighted = (sample_weight[None, :] * sketch).astype(jnp.bfloat16)
    positions = lax.broadcasted_iota(jnp.int32, block_values.shape, 4)
    masked = jnp.where(
        positions < block_count[..., None], block_values, jnp.zeros_like(block_values)
    )[0]
    tile_count = masked.shape[1]
    slot_count = masked.shape[2]
    weighted_rows = weighted.T
    picked = jnp.take(weighted_rows, block_sample.reshape(-1), axis=0)
    picked = picked.reshape(device_count, tile_count, slot_count, rank_width)
    values_in, rows_in = sent_together(
        (masked.reshape(device_count, -1), picked.reshape(device_count, -1)), ROW, 0, 0, 1
    )
    gathered = jnp.einsum(
        "stcr,stck->ktr",
        values_in.reshape(masked.shape),
        rows_in.reshape(picked.shape),
        preferred_element_type=jnp.float32,
    ).reshape(rank_width, -1)
    total_rows = gathered.shape[1] * device_count
    total_samples = sketch.shape[1] * device_count
    ridge = 0.05 * live_total / total_rows
    system = gram_matrix / total_samples + ridge * jnp.eye(rank_width, dtype=jnp.float32)
    lower_factor = jnp.linalg.cholesky(system)
    half_solved = lax.linalg.triangular_solve(lower_factor, gathered, left_side=True, lower=True)
    update = lax.linalg.triangular_solve(
        lower_factor, half_solved, left_side=True, lower=True, transpose_a=True
    )
    column_sums = over_copies(jnp.sum(update * update, axis=1), ROW)
    scales = jnp.sqrt(column_sums / total_rows + 1e-06)
    return ((update / scales[:, None]).astype(jnp.bfloat16), scales)


def solution(mesh):
    split = Mesh(mesh.devices.reshape(mesh.shape["groups"], 32, 2), ("groups", "row_0", "row_1"))
    return jax.shard_map(
        shards,
        mesh=split,
        in_specs=(
            P(None, GROUPS_ROW),
            P(None, GROUPS_ROW),
            P(GROUPS_ROW),
            P(None, GROUPS_ROW, None),
            P(GROUPS_ROW),
            P(GROUPS_ROW, None, None, None, None),
            P(GROUPS_ROW, None, None, None),
            P(GROUPS_ROW, None, None, None),
        ),
        out_specs=(P(None, GROUPS_ROW), P("groups")),
        check_vma=False,
    )
```

profile of v0, /device:TPU:44, one launch (start us, length us, event | category | flops | bytes accessed | tf_op | source)
XLA Modules:
  0.0 407.9 jit_solution(13769192548734777162)
XLA Ops:
  0.6 0.8 broadcast_subtract_fusion
  1.4 1.5 copy.61
  3.0 29.2 %gather_fusion.2 = bf16[8192,64]{1,0:T(8,128)(2,1)} fusion(bf16[64,4096]{0,1:T(8,128)(2,1)S(1)} %copy.61, s32[8192]{0:T(1024)S(1)} %fusion.11), kind=kCustom, calls=%fused_computation.1.clone | custom fusion | bytes 2129920 | tf_op jit(solution)/shard_map/jit(_take)/gather | solution.py:47
  32.2 5.8 %broadcast_select_fusion = bf16[8192,64]{1,0:T(8,128)(2,1)S(1)} fusion(bf16[8192,64]{1,0:T(8,128)(2,1)} %gather_fusion.2, pred[8192]{0:T(1024)(128)(4,1)S(1)} %compare_and_fusion), kind=kLoop, calls=%fused_computation.6 | loop fusion | flops 524288 | bytes 2105344 | tf_op jit(solution)/shard_map/jit(_take)/select_n | solution.py:47
  38.0 0.0 copy-start
  38.0 1.6 copy.62
  39.7 34.4 %all-to-all-start = ((bf16[64,64,128]{2,0,1:T(8,128)(2,1)}), bf16[64,64,128]{2,0,1:T(8,128)(2,1)S(1)}, u32[]{:S(2)}, u32[]{:S(2)}) async-start(bf16[64,64,128]{2,0,1:T(8,128)(2,1)} %copy.62), calls=%async_computation | async-start | bytes 2097152 | tf_op jit(solution)/shard_map/all_to_all | solution.py:48
  74.1 0.0 copy-start.2
  74.1 0.5 copy.60
  74.6 0.1 copy.67
  74.7 0.2 reshape.108
  74.9 0.1 copy.66
  75.0 0.2 broadcast_in_dim.37
  75.2 0.2 broadcast_in_dim.38
  75.4 0.0 copy-done.5
  75.4 0.1 copy.65
  75.6 0.3 fusion.1
  75.9 0.2 reshape_squeeze.3
  76.1 29.2 %gather_fusion.1 = bf16[8192,64]{1,0:T(8,128)(2,1)} fusion(bf16[64,4096]{0,1:T(8,128)(2,1)S(1)} %copy.60, s32[8192]{0:T(1024)S(1)} %fusion.12), kind=kCustom, calls=%fused_computation.clone | custom fusion | bytes 2129920 | tf_op jit(solution)/shard_map/jit(_take)/gather | solution.py:45
  105.4 0.0 copy-start.3
  105.4 77.8 %all-to-all-done = bf16[64,64,128]{2,0,1:T(8,128)(2,1)S(1)} async-done(((bf16[64,64,128]{2,0,1:T(8,128)(2,1)}), bf16[64,64,128]{2,0,1:T(8,128)(2,1)S(1)}, u32[]{:S(2)}, u32[]{:S(2)}) %all-to-all-start) | async-done | bytes 1048608 | tf_op jit(solution)/shard_map/all_to_all | solution.py:48
  183.2 2.4 copy.63
  185.6 10.4 %fusion = (bf16[8192,64]{1,0:T(8,128)(2,1)S(1)}, f32[64,8192]{0,1:T(8,128)}) fusion(f32[8192]{0:T(1024)S(1)} %copy-done.3, f32[64,64,128]{0,2,1:T(8,128)} %copy.63, bf16[8192,64]{1,0:T(8,128)(2,1)} %gather_fusion.1, pred[8192]{0:T(1024)(128)(4,1)S(1)} %compare_and_fusion.1), kind=kLoop, calls=%fused_computation.5 | loop fusion | flops 3145728 | bytes 6332416 | tf_op jit(solution)/shard_map/transpose | solution.py:62
  196.0 3.2 gather_fusion
  199.2 0.2 gather.10
  199.4 0.5 broadcast.154
  200.0 0.9 reduce.7
  200.8 1.0 reshape.144
  201.9 6.7 %all-to-all-start.1 = ((bf16[64,2,1536]{2,1,0:T(2,128)(2,1)}), bf16[64,2,1536]{2,1,0:T(2,128)(2,1)S(1)}, u32[]{:S(2)}, u32[]{:S(2)}) async-start(bf16[64,2,1536]{2,1,0:T(2,128)(2,1)} %reshape.144), calls=%async_computation.1 | async-start | bytes 786432 | tf_op jit(solution)/shard_map/all_to_all | solution.py:20
  208.5 0.6 convert_reduce_fusion
  209.1 10.4 %fusion.13 = f32[64,64]{1,0:T(8,128)S(1)} fusion(f32[64,8192]{0,1:T(8,128)} %get-tuple-element.8), kind=kOutput, calls=%fused_computation.44 | convolution fusion | flops 402653184 | bytes 2113536 | tf_op jit(solution)/shard_map/dot_general | solution.py:52
  219.6 125.4 %all-reduce = (f32[64,64]{1,0:T(8,128)S(1)}, f32[]{:T(128)}) all-reduce(f32[64,64]{1,0:T(8,128)S(1)} %fusion.13, f32[]{:T(128)} %convert_reduce_fusion), channel_id=1, replica_groups=mesh['groups'=4,'row_0'=32,'row_1'=2] {'row_0'}, use_global_device_ids=true, to_apply=%region_0.0 | all-reduce | flops 4097 | bytes 32776 | tf_op jit(solution)/shard_map/psum | solution.py:13
  345.0 4.6 %all-reduce.1 = (f32[64,64]{1,0:T(8,128)S(1)}, f32[]{:T(128)}) all-reduce(f32[64,64]{1,0:T(8,128)S(1)} %get-tuple-element.3, f32[]{:T(128)} %get-tuple-element.4), channel_id=1, replica_groups=mesh['groups'=4,'row_0'=32,'row_1'=2] {'row_1'}, use_global_device_ids=true, to_apply=%region_1.3 | all-reduce | flops 4097 | bytes 32776 | tf_op jit(solution)/shard_map/psum | solution.py:13
  350.2 0.1 copy.64
  350.3 5.8 %cholesky.16 = f32[64,64]{1,0:T(8,128)S(1)} custom-call(f32[64,64]{1,0:T(8,128)S(1)} %fusion.10), custom_call_target="Cholesky" | custom-call | tf_op jit(solution)/shard_map/jit(cholesky)/cholesky | solution.py:78
  356.2 0.6 compare_reduce_fusion
  356.8 0.7 fusion.6
  357.5 4.9 %custom-call.8 = f32[1,64,64]{1,2,0:T(8,128)S(1)} custom-call(f32[1,64,64]{2,1,0:T(8,128)S(1)} %fusion.6), custom_call_target="InvertDiagBlocksLowerTriangular" | custom-call | tf_op jit(solution)/shard_map/triangular_solve | solution.py:80
  362.4 0.0 all-to-all-done.1
  362.4 0.3 reshape.145
  362.8 0.1 copy.83
  363.0 0.2 reshape.110
  363.1 0.2 copy.69
  363.3 0.2 convolution_bitcast_fusion
  363.5 0.3 fusion.3
  363.9 0.4 multiply_reduce_fusion
  364.3 42.9 %all_to_all.23 = f32[64,1,64]{2,1,0:T(1,128)S(1)} all-to-all(f32[64,1,64]{2,1,0:T(1,128)S(1)} %broadcast_in_dim.40), channel_id=1, replica_groups=mesh['groups'=4,'row_0'=32,'row_1'=2] {'row_0','row_1'}, dimensions={0} | all-to-all | bytes 32768 | tf_op jit(solution)/shard_map/all_to_all | solution.py:32
  407.2 0.7 divide_convert_fusion
  (27 shorter events, 0.3 us)
Async XLA Ops:
  38.0 36.0 %copy-start = (bf16[64,4096]{1,0:T(8,128)(2,1)S(1)}, bf16[64,4096]{1,0:T(8,128)(2,1)}, u32[]{:S(2)}) copy-start(bf16[64,4096]{1,0:T(8,128)(2,1)} %param.10) | copy-start | bytes 1572868
  39.7 34.9 %copy-start.4 = (s32[1,64,4,4]{1,3,2,0:T(4,128)S(1)}, s32[1,64,4,4]{1,3,2,0:T(4,128)}, u32[]{:S(2)}) copy-start(s32[1,64,4,4]{1,3,2,0:T(4,128)} %param.16) | copy-start | bytes 12292
  39.7 35.7 %copy-start.5 = (s32[1,64,4,4]{1,3,2,0:T(4,128)S(1)}, s32[1,64,4,4]{1,3,2,0:T(4,128)}, u32[]{:S(2)}) copy-start(s32[1,64,4,4]{1,3,2,0:T(4,128)} %param.17) | copy-start | bytes 12292
  39.7 35.9 %copy-start.1 = (bf16[1,64,4,4,128]{4,3,2,1,0:T(4,128)(2,1)S(1)}, bf16[1,64,4,4,128]{4,3,2,1,0:T(4,128)(2,1)}, u32[]{:S(2)}) copy-start(bf16[1,64,4,4,128]{4,3,2,1,0:T(4,128)(2,1)} %param.15) | copy-start | bytes 786436
  39.7 143.5 %all-to-all-start = ((bf16[64,64,128]{2,0,1:T(8,128)(2,1)}), bf16[64,64,128]{2,0,1:T(8,128)(2,1)S(1)}, u32[]{:S(2)}, u32[]{:S(2)}) async-start(bf16[64,64,128]{2,0,1:T(8,128)(2,1)} %copy.62), calls=%async_computation | async-start | bytes 2097152 | tf_op jit(solution)/shard_map/all_to_all | solution.py:48
  74.1 2.0 copy-start.2
  105.4 80.2 %copy-start.3 = (f32[8192]{0:T(1024)S(1)}, f32[8192]{0:T(1024)}, u32[]{:S(2)}) copy-start(f32[8192]{0:T(1024)} %param.14) | copy-start | bytes 98308
  201.9 160.5 %all-to-all-start.1 = ((bf16[64,2,1536]{2,1,0:T(2,128)(2,1)}), bf16[64,2,1536]{2,1,0:T(2,128)(2,1)S(1)}, u32[]{:S(2)}, u32[]{:S(2)}) async-start(bf16[64,2,1536]{2,1,0:T(2,128)(2,1)} %reshape.144), calls=%async_computation.1 | async-start | bytes 786432 | tf_op jit(solution)/shard_map/all_to_all | solution.py:20
  407.2 0.7 copy-start.6
where the time goes:
time: 409 us; the launch traced here: 408 us
  blocking collectives  173 us (42%)
  waiting for transfers between devices  77.8 us (19%)
  local copies, waits for them, and re-layouts  71.5 us (17%)
  starting transfers between devices  41 us (10%)
  other arithmetic  31.7 us (8%)
  matrix products  11.3 us (3%)
    psum x2, blocking collectives, by_axis(): x = lax.psum(x, axis)  130 us
    all_to_all x1, waiting for transfers between devices, shards(): lax.all_to_all(c_outgoing, ROW, split_axis=1, concat_axis=1, tiled=True)  77.8 us
    all_to_all x1, blocking collectives, from_everyone(): lax.all_to_all(jnp.broadcast_to(x[None], (devices, *x.shape)), axis, 0, 0...  42.9 us
    all_to_all x1, starting transfers between devices, shards(): lax.all_to_all(c_outgoing, ROW, split_axis=1, concat_axis=1, tiled=True)  34.4 us
    gather x1, local copies, waits for them, and re-layouts, shards(): jnp.take(factor_c, c_local, axis=1).reshape(rank_width, device_count, -1)  29.2 us
    gather x1, local copies, waits for them, and re-layouts, shards(): jnp.take(factor_b, sample_j - device_index * factor_b.shape[1], axis=1)  29.2 us
    dot_general x1, matrix products, shards(): gram_local = jnp.dot(sketch, sketch.T, precision=lax.Precision.HIGHEST)  10.4 us
    transpose x1, other arithmetic, shards(): weighted_rows = weighted.T  10.4 us
  transfers between devices with their start and end apart: 2, of which 1 were waited for; matrix products, arithmetic and copies ran while one was open for 13% of the time, Pallas kernels for 0%

commit v1 on v0

--- a/solution.py
+++ b/solution.py
@@ -10,7 +10,7 @@
 
 def by_axis(x, axes):
     for axis in axes:
-        x = lax.psum(x, axis)
+        x = jnp.sum(lax.all_gather(x, axis), axis=0)
     return x
 
 

time: 409 us -> 429 us (1.049)
  blocking collectives: 173 us -> 188 us
    psum x2 -> x0, blocking collectives: 130 us -> none  [by_axis(): x = lax.psum(x, axis)]
    unnamed x0 -> x2, blocking collectives: none -> 85.5 us
    all_gather x0 -> x2, blocking collectives: none -> 60.1 us  [by_axis(): x = jnp.sum(lax.all_gather(x, axis), axis=0)]
  transfers between devices with their start and end apart: 2 -> 2, of which waited for: 1 -> 1; matrix products, arithmetic and copies ran while one was open for 13% -> 14% of each run, Pallas kernels for 0% -> 0%
where the time goes in v1:
time: 429 us
  blocking collectives  188 us (44%)
  waiting for transfers between devices  77.8 us (18%)
  local copies, waits for them, and re-layouts  75.5 us (18%)
  starting transfers between devices  40.8 us (10%)
  other arithmetic  33 us (8%)
  matrix products  11.3 us (3%)
    unnamed x2, blocking collectives  85.5 us
    all_to_all x1, waiting for transfers between devices, shards(): lax.all_to_all(c_outgoing, ROW, split_axis=1, concat_axis=1, tiled=True)  77.8 us
    all_gather x2, blocking collectives, by_axis(): x = jnp.sum(lax.all_gather(x, axis), axis=0)  60.1 us
    all_to_all x1, blocking collectives, from_everyone(): lax.all_to_all(jnp.broadcast_to(x[None], (devices, *x.shape)), axis, 0, 0...  42.6 us
    all_to_all x1, starting transfers between devices, shards(): lax.all_to_all(c_outgoing, ROW, split_axis=1, concat_axis=1, tiled=True)  34.4 us
    gather x1, local copies, waits for them, and re-layouts, shards(): jnp.take(factor_c, c_local, axis=1).reshape(rank_width, device_count, -1)  29.2 us
    gather x1, local copies, waits for them, and re-layouts, shards(): jnp.take(factor_b, sample_j - device_index * factor_b.shape[1], axis=1)  29.2 us
    dot_general x1, matrix products, shards(): gram_local = jnp.dot(sketch, sketch.T, precision=lax.Precision.HIGHEST)  10.4 us
  transfers between devices with their start and end apart: 2, of which 1 were waited for; matrix products, arithmetic and copies ran while one was open for 14% of the time, Pallas kernels for 0%

profile of v1, /device:TPU:44, one launch (start us, length us, event | category | flops | bytes accessed | tf_op | source)
XLA Modules:
  0.0 428.5 jit_solution(14390687176545572438)
XLA Ops:
  0.6 0.8 broadcast_subtract_fusion
  1.4 1.5 copy.62
  3.0 29.2 %gather_fusion.2 = bf16[8192,64]{1,0:T(8,128)(2,1)} fusion(bf16[64,4096]{0,1:T(8,128)(2,1)S(1)} %copy.62, s32[8192]{0:T(1024)S(1)} %fusion.12), kind=kCustom, calls=%fused_computation.1.clone | custom fusion | bytes 2129920 | tf_op jit(solution)/shard_map/jit(_take)/gather | solution.py:47
  32.2 5.8 %broadcast_select_fusion = bf16[8192,64]{1,0:T(8,128)(2,1)S(1)} fusion(bf16[8192,64]{1,0:T(8,128)(2,1)} %gather_fusion.2, pred[8192]{0:T(1024)(128)(4,1)S(1)} %compare_and_fusion), kind=kLoop, calls=%fused_computation.6 | loop fusion | flops 524288 | bytes 2105344 | tf_op jit(solution)/shard_map/jit(_take)/select_n | solution.py:47
  38.0 1.6 copy.63
  39.7 34.4 %all-to-all-start = ((bf16[64,64,128]{2,0,1:T(8,128)(2,1)}), bf16[64,64,128]{2,0,1:T(8,128)(2,1)S(1)}, u32[]{:S(2)}, u32[]{:S(2)}) async-start(bf16[64,64,128]{2,0,1:T(8,128)(2,1)} %copy.63), calls=%async_computation | async-start | bytes 2097152 | tf_op jit(solution)/shard_map/all_to_all | solution.py:48
  74.1 0.5 copy.61
  74.6 0.1 copy.69
  74.7 0.2 reshape.108
  75.0 0.2 broadcast_in_dim.37
  75.2 0.2 broadcast_in_dim.38
  75.6 0.3 fusion.1
  75.9 0.2 reshape_squeeze.3
  76.1 29.2 %gather_fusion.1 = bf16[8192,64]{1,0:T(8,128)(2,1)} fusion(bf16[64,4096]{0,1:T(8,128)(2,1)S(1)} %copy.61, s32[8192]{0:T(1024)S(1)} %fusion.13), kind=kCustom, calls=%fused_computation.clone | custom fusion | bytes 2129920 | tf_op jit(solution)/shard_map/jit(_take)/gather | solution.py:45
  105.4 77.8 %all-to-all-done = bf16[64,64,128]{2,0,1:T(8,128)(2,1)S(1)} async-done(((bf16[64,64,128]{2,0,1:T(8,128)(2,1)}), bf16[64,64,128]{2,0,1:T(8,128)(2,1)S(1)}, u32[]{:S(2)}, u32[]{:S(2)}) %all-to-all-start) | async-done | bytes 1048608 | tf_op jit(solution)/shard_map/all_to_all | solution.py:48
  183.2 2.4 copy.64
  185.6 10.4 %fusion = (bf16[8192,64]{1,0:T(8,128)(2,1)S(1)}, f32[64,8192]{0,1:T(8,128)}) fusion(f32[8192]{0:T(1024)S(1)} %copy-done.3, f32[64,64,128]{0,2,1:T(8,128)} %copy.64, bf16[8192,64]{1,0:T(8,128)(2,1)} %gather_fusion.1, pred[8192]{0:T(1024)(128)(4,1)S(1)} %compare_and_fusion.1), kind=kLoop, calls=%fused_computation.5 | loop fusion | flops 3145728 | bytes 6332416 | tf_op jit(solution)/shard_map/transpose | solution.py:62
  196.0 3.2 gather_fusion
  199.2 0.2 gather.10
  199.5 0.5 broadcast.159
  200.0 0.9 reduce.9
  200.9 1.0 reshape.156
  201.9 6.5 %all-to-all-start.1 = ((bf16[64,2,1536]{2,1,0:T(2,128)(2,1)}), bf16[64,2,1536]{2,1,0:T(2,128)(2,1)S(1)}, u32[]{:S(2)}, u32[]{:S(2)}) async-start(bf16[64,2,1536]{2,1,0:T(2,128)(2,1)} %reshape.156), calls=%async_computation.1 | async-start | bytes 786432 | tf_op jit(solution)/shard_map/all_to_all | solution.py:20
  208.4 0.6 dynamic-slice
  209.0 0.6 convert_reduce_fusion
  209.6 1.4 dynamic-update-slice.3
  211.0 82.9 %all-reduce = f32[32]{0:T(128)S(1)} all-reduce(f32[32]{0:T(128)S(1)} %dynamic-update-slice.3), channel_id=1, replica_groups=mesh['groups'=4,'row_0'=32,'row_1'=2] {'row_0'}, use_global_device_ids=true, to_apply=%add | all-reduce | flops 32 | bytes 256
  293.9 0.6 reduce_sum.66
  294.5 0.6 dynamic-slice.1
  295.0 1.4 dynamic-update-slice.4
  296.5 2.7 all-reduce.1
  299.1 0.6 reduce_sum.67
  300.4 10.4 %fusion.14 = f32[64,64]{1,0:T(8,128)S(1)} fusion(f32[64,8192]{0,1:T(8,128)} %get-tuple-element.4), kind=kOutput, calls=%fused_computation.46 | convolution fusion | flops 402653184 | bytes 2113536 | tf_op jit(solution)/shard_map/dot_general | solution.py:52
  310.8 58.2 %all-gather = f32[2048,64]{1,0:T(8,128)S(1)} all-gather(f32[64,64]{1,0:T(8,128)S(1)} %fusion.14), channel_id=2, replica_groups=mesh['groups'=4,'row_0'=32,'row_1'=2] {'row_0'}, dimensions={0}, use_global_device_ids=true | all-gather | bytes 540672 | tf_op jit(solution)/shard_map/all_gather | solution.py:13
  369.1 1.9 all-gather.1
  371.2 5.8 %cholesky.16 = f32[64,64]{1,0:T(8,128)S(1)} custom-call(f32[64,64]{1,0:T(8,128)S(1)} %fusion.11), custom_call_target="Cholesky" | custom-call | tf_op jit(solution)/shard_map/jit(cholesky)/cholesky | solution.py:78
  377.1 0.6 compare_reduce_fusion
  377.7 0.7 fusion.6
  378.4 4.9 %custom-call.8 = f32[1,64,64]{1,2,0:T(8,128)S(1)} custom-call(f32[1,64,64]{2,1,0:T(8,128)S(1)} %fusion.6), custom_call_target="InvertDiagBlocksLowerTriangular" | custom-call | tf_op jit(solution)/shard_map/triangular_solve | solution.py:80
  383.3 0.3 reshape.157
  383.7 0.1 copy.85
  383.8 0.2 reshape.110
  384.0 0.2 copy.71
  384.2 0.2 convolution_bitcast_fusion
  384.4 0.3 fusion.3
  384.8 0.4 multiply_reduce_fusion
  385.1 42.6 %all_to_all.23 = f32[64,1,64]{2,1,0:T(1,128)S(1)} all-to-all(f32[64,1,64]{2,1,0:T(1,128)S(1)} %broadcast_in_dim.40), channel_id=1, replica_groups=mesh['groups'=4,'row_0'=32,'row_1'=2] {'row_0','row_1'}, dimensions={0} | all-to-all | bytes 32768 | tf_op jit(solution)/shard_map/all_to_all | solution.py:32
  427.8 0.7 divide_convert_fusion
  (44 shorter events, 0.8 us)
Async XLA Ops:
  38.0 36.0 %copy-start = (bf16[64,4096]{1,0:T(8,128)(2,1)S(1)}, bf16[64,4096]{1,0:T(8,128)(2,1)}, u32[]{:S(2)}) copy-start(bf16[64,4096]{1,0:T(8,128)(2,1)} %param.10) | copy-start | bytes 1572868
  39.7 34.9 %copy-start.4 = (s32[1,64,4,4]{1,3,2,0:T(4,128)S(1)}, s32[1,64,4,4]{1,3,2,0:T(4,128)}, u32[]{:S(2)}) copy-start(s32[1,64,4,4]{1,3,2,0:T(4,128)} %param.16) | copy-start | bytes 12292
  39.7 35.7 %copy-start.5 = (s32[1,64,4,4]{1,3,2,0:T(4,128)S(1)}, s32[1,64,4,4]{1,3,2,0:T(4,128)}, u32[]{:S(2)}) copy-start(s32[1,64,4,4]{1,3,2,0:T(4,128)} %param.17) | copy-start | bytes 12292
  39.7 35.9 %copy-start.1 = (bf16[1,64,4,4,128]{4,3,2,1,0:T(4,128)(2,1)S(1)}, bf16[1,64,4,4,128]{4,3,2,1,0:T(4,128)(2,1)}, u32[]{:S(2)}) copy-start(bf16[1,64,4,4,128]{4,3,2,1,0:T(4,128)(2,1)} %param.15) | copy-start | bytes 786436
  39.7 143.5 %all-to-all-start = ((bf16[64,64,128]{2,0,1:T(8,128)(2,1)}), bf16[64,64,128]{2,0,1:T(8,128)(2,1)S(1)}, u32[]{:S(2)}, u32[]{:S(2)}) async-start(bf16[64,64,128]{2,0,1:T(8,128)(2,1)} %copy.63), calls=%async_computation | async-start | bytes 2097152 | tf_op jit(solution)/shard_map/all_to_all | solution.py:48
  74.1 2.0 copy-start.2
  105.4 80.2 %copy-start.3 = (f32[8192]{0:T(1024)S(1)}, f32[8192]{0:T(1024)}, u32[]{:S(2)}) copy-start(f32[8192]{0:T(1024)} %param.14) | copy-start | bytes 98308
  199.2 9.2 %copy-start.8 = (u32[256]{0:T(256)S(1)}, u32[256]{0:T(256)}, u32[]{:S(2)}) copy-start(u32[256]{0:T(256)} %constant.106) | copy-start | bytes 3076
  199.2 95.3 %copy-start.7 = (u32[256]{0:T(256)S(1)}, u32[256]{0:T(256)}, u32[]{:S(2)}) copy-start(u32[256]{0:T(256)} %constant.111) | copy-start | bytes 3076
  201.9 181.4 %all-to-all-start.1 = ((bf16[64,2,1536]{2,1,0:T(2,128)(2,1)}), bf16[64,2,1536]{2,1,0:T(2,128)(2,1)S(1)}, u32[]{:S(2)}, u32[]{:S(2)}) async-start(bf16[64,2,1536]{2,1,0:T(2,128)(2,1)} %reshape.156), calls=%async_computation.1 | async-start | bytes 786432 | tf_op jit(solution)/shard_map/all_to_all | solution.py:20
  427.8 0.7 copy-start.6
